TPU v7x, 256 devices: a whole 4x4x8 slice. The times are simulated.
256 devices in a mesh: expert: 8 (over x, core), shard: 32 (over z, y).
Axes of the slice: x: 4, y: 4, z: 8, core: 2. Of those that a mesh axis runs over, the one named last changes fastest.
Arguments:
- train_down: float32 [16, 6400, 4096], P('expert', None, 'shard'), may hold values from -0.15625 to 0.15625
- other_down: bfloat16 [16, 6400, 4096], P('expert', None, 'shard'), may hold values from -0.0390625 to 0.0390625
- router_weight: float32 [4096, 16], P('shard', 'expert'), may hold values from -0.09375 to 0.09375
- router_gain: float32 [4096], P('shard'), may hold values from 0.25 to 1.75
Outputs:
- ready_down: bfloat16 [16, 6400, 4096], P('expert', 'shard')
- scale_down: float32 [16, 6400], P('expert', 'shard')
- serve_router: bfloat16 [4096, 16], replicated
All inputs are finite; a program needn't handle non-finite values. Where the computation divides by a largest or mean magnitude, that divisor is 1e-20 or more.
Results may differ from a plain program's by a relative error of at most 0.001.
Values may be sent and summed in bfloat16 or wider, within the bound.
A program may use at most 64 MiB of HBM per device.

v0:
```python
import jax
import jax.numpy as jnp
from jax import lax
from jax.sharding import PartitionSpec as P


def sent_to_all(x, axis):
    copies = jnp.broadcast_to(x, (lax.axis_size(axis), *x.shape))
    return lax.all_to_all(copies, axis, split_axis=0, concat_axis=0, tiled=True)


def of_everyone(x, axis):
    everything = sent_to_all(x, axis)
    return jnp.max(everything, axis=0)


def laid_out(parts, dim):
    lengths = list(parts.shape[1:])
    lengths[dim] *= parts.shape[0]
    return jnp.moveaxis(parts, 0, dim).reshape(lengths)


def gathered_copies(x, axis, dim):
    return laid_out(sent_to_all(x, axis), dim)


def per_device(train_down, other_down, router_weight, router_gain):
    latest_down = train_down + other_down.astype(jnp.float32)
    scale_down = of_everyone(jnp.max(jnp.abs(latest_down), axis=2), "shard")
    narrow_down = (latest_down / jnp.expand_dims(scale_down, 2)).astype(jnp.bfloat16)
    ready_down = lax.all_to_all(narrow_down, "shard", split_axis=1, concat_axis=2, tiled=True)
    scale_down = lax.dynamic_slice_in_dim(
        scale_down, lax.axis_index("shard") * ready_down.shape[1], ready_down.shape[1], axis=1
    )
    part_router = (router_weight * router_gain[:, None]).astype(jnp.bfloat16)
    row_router = gathered_copies(part_router, "shard", 0)
    serve_router = gathered_copies(row_router, "expert", 1)
    return (ready_down, scale_down, serve_router)


def solution(mesh):
    in_specs = (
        P("expert", None, "shard"),
        P("expert", None, "shard"),
        P("shard", "expert"),
        P("shard"),
    )
    out_specs = (P("expert", "shard", None), P("expert", "shard"), P())
    return jax.shard_map(
        per_device, mesh=mesh, in_specs=in_specs, out_specs=out_specs, check_vma=False
    )
```

profile of v0, /device:TPU:24, one launch (start us, length us, event | category | flops | bytes accessed | tf_op | source)
XLA Modules:
  0.0 200.3 jit_solution(1283728771421727400)
XLA Ops:
  0.6 0.7 multiply_convert_fusion
  1.3 0.6 broadcast_in_dim.12
  1.9 11.5 %all-to-all-start.2 = ((bf16[32,128,2]{1,2,0:T(2,128)(2,1)}), bf16[32,128,2]{1,2,0:T(2,128)(2,1)S(1)}, u32[]{:S(2)}, u32[]{:S(2)}) async-start(bf16[32,128,2]{1,2,0:T(2,128)(2,1)} %broadcast_in_dim.12), calls=%async_computation.2 | async-start | bytes 32768 | tf_op jit(solution)/shard_map/all_to_all | solution.py:9
  13.4 5.6 %abs_reduce_fusion = f32[2,6400]{1,0:T(2,128)S(1)} fusion(f32[2,6400,128]{2,1,0:T(8,128)} %param.4, bf16[2,6400,128]{2,1,0:T(8,128)(2,1)} %param.5), kind=kLoop, calls=%fused_computation.1 | loop fusion | flops 6540800 | bytes 9881600 | tf_op jit(solution)/shard_map/reduce_max | solution.py:29
  19.0 0.0 copy-start
  19.0 2.3 %all-to-all-done.2 = bf16[32,128,2]{1,2,0:T(2,128)(2,1)S(1)} async-done(((bf16[32,128,2]{1,2,0:T(2,128)(2,1)}), bf16[32,128,2]{1,2,0:T(2,128)(2,1)S(1)}, u32[]{:S(2)}, u32[]{:S(2)}) %all-to-all-start.2) | async-done | bytes 16416 | tf_op jit(solution)/shard_map/all_to_all | solution.py:9
  21.3 0.4 broadcast_in_dim.11
  21.8 47.7 %all_to_all.33 = f32[32,2,6400]{2,1,0:T(2,128)} all-to-all(f32[32,2,6400]{2,1,0:T(2,128)S(1)} %broadcast_in_dim.11), channel_id=1, replica_groups=mesh['expert'=8,'shard'=32] {'shard'}, dimensions={0} | all-to-all | bytes 3276800 | tf_op jit(solution)/shard_map/all_to_all | solution.py:9
  69.4 0.7 broadcast_in_dim.13
  70.2 4.3 %all-to-all-start.3 = ((bf16[8,4096,2]{1,2,0:T(2,128)(2,1)}), bf16[8,4096,2]{1,2,0:T(2,128)(2,1)S(1)}, u32[]{:S(2)}, u32[]{:S(2)}) async-start(bf16[8,4096,2]{1,2,0:T(2,128)(2,1)} %broadcast_in_dim.13), calls=%async_computation.3 | async-start | bytes 262144 | tf_op jit(solution)/shard_map/all_to_all | solution.py:9
  74.5 1.9 reduce_max.19
  76.4 0.0 copy-done
  76.4 4.7 %divide_convert_fusion = bf16[2,6400,128]{2,1,0:T(8,128)(2,1)S(1)} fusion(f32[2,6400,128]{2,1,0:T(8,128)} %param.4, bf16[2,6400,128]{2,1,0:T(8,128)(2,1)S(1)} %copy-done, f32[2,6400]{1,0:T(2,128)S(1)} %reduce_max.19), kind=kLoop, calls=%fused_computation | loop fusion | flops 6553600 | bytes 13158400 | tf_op jit(solution)/shard_map/convert_element_type | solution.py:30
  81.1 27.9 %copy.31 = bf16[2,6400,128]{2,0,1:T(2,128)(2,1)} copy(bf16[2,6400,128]{2,1,0:T(8,128)(2,1)S(1)} %divide_convert_fusion) | data formatting | bytes 6553600 | tf_op jit(solution)/shard_map/convert_element_type | solution.py:30
  109.0 0.0 all-to-all-done.3
  109.0 5.6 %all-to-all-start.1 = ((bf16[2,6400,128]{2,0,1:T(2,128)(2,1)}), bf16[2,6400,128]{2,0,1:T(2,128)(2,1)S(1)}, u32[]{:S(2)}, u32[]{:S(2)}) async-start(bf16[2,6400,128]{2,0,1:T(2,128)(2,1)} %copy.31), calls=%async_computation.1 | async-start | bytes 6553600 | tf_op jit(solution)/shard_map/all_to_all | solution.py:31
  114.6 0.7 reshape.15
  115.3 0.7 constant_dynamic-slice_fusion
  115.9 75.6 %all-to-all-done.1 = bf16[2,6400,128]{2,0,1:T(2,128)(2,1)S(1)} async-done(((bf16[2,6400,128]{2,0,1:T(2,128)(2,1)}), bf16[2,6400,128]{2,0,1:T(2,128)(2,1)S(1)}, u32[]{:S(2)}, u32[]{:S(2)}) %all-to-all-start.1) | async-done | bytes 3276832 | tf_op jit(solution)/shard_map/all_to_all | solution.py:31
  191.6 2.5 %copy.32 = bf16[2,200,32,128]{3,2,1,0:T(8,128)(2,1)} copy(bf16[2,200,32,128]{3,0,1,2:T(2,128)(2,1)S(1)} %bitcast.9) | data formatting | bytes 6553600 | tf_op jit(solution)/shard_map/all_to_all | solution.py:31
  194.1 6.2 %all_to_all.26 = bf16[2,200,4096]{2,1,0:T(8,128)(2,1)} reshape(bf16[2,200,32,128]{3,2,1,0:T(8,128)(2,1)} %copy.32) | data formatting | bytes 6553600 | tf_op jit(solution)/shard_map/all_to_all | solution.py:31
Async XLA Ops:
  1.9 19.4 %all-to-all-start.2 = ((bf16[32,128,2]{1,2,0:T(2,128)(2,1)}), bf16[32,128,2]{1,2,0:T(2,128)(2,1)S(1)}, u32[]{:S(2)}, u32[]{:S(2)}) async-start(bf16[32,128,2]{1,2,0:T(2,128)(2,1)} %broadcast_in_dim.12), calls=%async_computation.2 | async-start | bytes 32768 | tf_op jit(solution)/shard_map/all_to_all | solution.py:9
  19.0 57.4 %copy-start = (bf16[2,6400,128]{2,1,0:T(8,128)(2,1)S(1)}, bf16[2,6400,128]{2,1,0:T(8,128)(2,1)}, u32[]{:S(2)}) copy-start(bf16[2,6400,128]{2,1,0:T(8,128)(2,1)} %param.5) | copy-start | bytes 9830404
  70.2 38.8 %all-to-all-start.3 = ((bf16[8,4096,2]{1,2,0:T(2,128)(2,1)}), bf16[8,4096,2]{1,2,0:T(2,128)(2,1)S(1)}, u32[]{:S(2)}, u32[]{:S(2)}) async-start(bf16[8,4096,2]{1,2,0:T(2,128)(2,1)} %broadcast_in_dim.13), calls=%async_computation.3 | async-start | bytes 262144 | tf_op jit(solution)/shard_map/all_to_all | solution.py:9
  109.0 82.6 %all-to-all-start.1 = ((bf16[2,6400,128]{2,0,1:T(2,128)(2,1)}), bf16[2,6400,128]{2,0,1:T(2,128)(2,1)S(1)}, u32[]{:S(2)}, u32[]{:S(2)}) async-start(bf16[2,6400,128]{2,0,1:T(2,128)(2,1)} %copy.31), calls=%async_computation.1 | async-start | bytes 6553600 | tf_op jit(solution)/shard_map/all_to_all | solution.py:31
where the time goes:
time: 202 us; the launch traced here: 200 us
  waiting for transfers between devices  77.9 us (39%)
  blocking collectives  47.7 us (24%)
  local copies, waits for them, and re-layouts  39.7 us (20%)
  starting transfers between devices  21.3 us (11%)
  other arithmetic  12.9 us (6%)
    all_to_all x1, waiting for transfers between devices, per_device(): lax.all_to_all(narrow_down, 'shard', split_axis=1, concat_axis=2, tiled=T...  75.6 us
    all_to_all x1, blocking collectives, sent_to_all(): return lax.all_to_all(copies, axis, split_axis=0, concat_axis=0, tiled=True)  47.7 us
    convert_element_type x1, local copies, waits for them, and re-layouts, per_device(): (latest_down / jnp.expand_dims(scale_down, 2)).astype(jnp.bfloat16)  27.9 us
    all_to_all x2, starting transfers between devices, sent_to_all(): return lax.all_to_all(copies, axis, split_axis=0, concat_axis=0, tiled=True)  15.8 us
    all_to_all x2, local copies, waits for them, and re-layouts, per_device(): lax.all_to_all(narrow_down, 'shard', split_axis=1, concat_axis=2, tiled=T...  8.72 us
    reduce_max x1, other arithmetic, per_device(): scale_down = of_everyone(jnp.max(jnp.abs(latest_down), axis=2), 'shard')  5.6 us
    all_to_all x1, starting transfers between devices, per_device(): lax.all_to_all(narrow_down, 'shard', split_axis=1, concat_axis=2, tiled=T...  5.57 us
    convert_element_type x1, other arithmetic, per_device(): (latest_down / jnp.expand_dims(scale_down, 2)).astype(jnp.bfloat16)  4.74 us
  transfers between devices with their start and end apart: 3, of which 2 were waited for; matrix products, arithmetic and copies ran while one was open for 21% of the time, Pallas kernels for 0%

commit v1 on v0

v1 whole, which is shorter than its diff:
```python
import functools

import jax
import jax.numpy as jnp
from jax import lax
from jax.experimental import pallas as pl
from jax.experimental.pallas import tpu as pltpu
from jax.sharding import PartitionSpec as P

MESH = pl.DeviceIdType.MESH
NZ, NY = 8, 4
LANES = 128


def peer_of(me, k):
    h = (k // NY + 1) // 2
    dz = h * (2 * ((k // NY) % 2) - 1)
    return ((me // NY + dz + NZ) % NZ) * NY + (me % NY + k) % NY


def exchange(train, other, weight, gain, out, scale, router,
             latest, late, sendbuf, maxima, seen, whole, scales,
             load_sem, m_send, m_recv, s_send, s_recv, d_send, d_recv, r_send, r_recv, e_send, e_recv):
    me, ex = lax.axis_index("shard"), lax.axis_index("expert")
    shards, experts = lax.axis_size("shard"), lax.axis_size("expert")
    rows = train.shape[1] // shards
    second = rows - LANES
    chunks = load_sem.shape[1]
    chunk = train.shape[1] // chunks

    barrier = pltpu.get_barrier_semaphore()

    def greet(k, c):
        pl.semaphore_signal(barrier, inc=1, device_id={"shard": (me + k) % shards}, device_id_type=MESH)
        return c

    lax.fori_loop(1, shards, greet, 0)

    def greet_expert(k, c):
        pl.semaphore_signal(barrier, inc=1, device_id={"expert": (ex + k) % experts}, device_id_type=MESH)
        return c

    lax.fori_loop(1, experts, greet_expert, 0)

    loads = []
    for c in range(chunks):
        at = pl.ds(c * chunk, chunk)
        a = pltpu.make_async_copy(train.at[:, at], latest.at[:, at], load_sem.at[0, c])
        b = pltpu.make_async_copy(other.at[:, at], late.at[:, at], load_sem.at[1, c])
        a.start()
        b.start()
        loads.append((a, b))

    part = (weight[...] * gain[...]).astype(jnp.bfloat16)
    mine = pl.ds(pl.multiple_of(me * LANES, LANES), LANES)
    router[ex, :, mine] = part

    def block_max(d, j):
        start = pl.multiple_of(d * rows + (second if j % 2 else 0), 8)
        x = jnp.abs(latest[j // 2, pl.ds(start, LANES), :])
        return jnp.max(x.T, axis=0, keepdims=True)

    for c in range(chunks):
        for load in loads[c]:
            load.wait()
        step = 160

        def add(i, carry):
            at = pl.ds(pl.multiple_of(c * chunk + i * step, 32), step)
            for e in range(2):
                latest[e, at, :] = latest[e, at, :] + late[e, at, :].astype(jnp.float32)
            return carry

        lax.fori_loop(0, chunk // step, add, 0)

        def one(d, carry):
            for j in range(4):
                maxima[d, j:j + 1, :] = block_max(d, j)
            return carry

        lax.fori_loop(c * chunk // rows, (c + 1) * chunk // rows, one, 0)

    pl.semaphore_wait(barrier, shards + experts - 2)

    def max_copy(d):
        return pltpu.make_async_remote_copy(
            maxima.at[d], seen.at[me], m_send.at[d], m_recv.at[me], device_id={"shard": d}, device_id_type=MESH)

    def max_from(s):
        return pltpu.make_async_remote_copy(
            maxima.at[s], seen.at[s], m_send.at[s], m_recv.at[s], device_id={"shard": s}, device_id_type=MESH)

    def send_max(k, c):
        max_copy(peer_of(me, shards - k)).start()
        return c

    lax.fori_loop(1, shards, send_max, 0)
    seen[me] = maxima[me]

    def router_copy(d):
        return pltpu.make_async_remote_copy(
            router.at[ex, :, mine], router.at[ex, :, mine], r_send.at[d], r_recv.at[me],
            device_id={"shard": d}, device_id_type=MESH)

    def router_from(s):
        at = pl.ds(pl.multiple_of(s * LANES, LANES), LANES)
        return pltpu.make_async_remote_copy(
            router.at[ex, :, at], router.at[ex, :, at], r_send.at[s], r_recv.at[s],
            device_id={"shard": s}, device_id_type=MESH)

    def wait_max(k, c):
        max_from(peer_of(me, k)).wait_recv()
        return c

    lax.fori_loop(1, shards, wait_max, 0)
    whole[...] = jnp.max(seen[...], axis=0)

    def scale_copy(d):
        return pltpu.make_async_remote_copy(
            whole, scales.at[me], s_send.at[d], s_recv.at[me], device_id={"shard": d}, device_id_type=MESH)

    def scale_from(s):
        return pltpu.make_async_remote_copy(
            whole, scales.at[s], s_send.at[s], s_recv.at[s], device_id={"shard": s}, device_id_type=MESH)

    def send_scale(k, c):
        scale_copy(peer_of(me, k)).start()
        return c

    lax.fori_loop(1, shards, send_scale, 0)
    scales[me] = whole[...]
    for e in range(2):
        scale[e:e + 1, 0:LANES] = whole[2 * e:2 * e + 1, :]
        scale[e:e + 1, LANES:rows] = whole[2 * e + 1:2 * e + 2, LANES - second:LANES]

    def send_router(k, c):
        router_copy(peer_of(me, k)).start()
        return c

    lax.fori_loop(1, shards, send_router, 0)

    def ready(d, j):
        column = jnp.broadcast_to(1.0 / scales[d, j:j + 1, :], (LANES, LANES)).T
        if j % 2:
            start, column = d * rows + LANES, column[LANES - second:]
        else:
            start = d * rows
        return latest[j // 2, pl.ds(pl.multiple_of(start, 8), column.shape[0]), :] * column

    def data_copy(d):
        return pltpu.make_async_remote_copy(
            sendbuf.at[d], out.at[:, :, mine], d_send.at[d], d_recv.at[me], device_id={"shard": d}, device_id_type=MESH)

    def data_from(s):
        at = pl.ds(pl.multiple_of(s * LANES, LANES), LANES)
        return pltpu.make_async_remote_copy(
            sendbuf.at[s], out.at[:, :, at], d_send.at[s], d_recv.at[s], device_id={"shard": s}, device_id_type=MESH)

    def prepare(d):
        for j in range(4):
            x = ready(d, j).astype(jnp.bfloat16)
            first = LANES if j % 2 else 0
            sendbuf[d, j // 2, first:first + x.shape[0], :] = x

    def send_data(k, c):
        d = peer_of(me, k)
        scale_from(d).wait_recv()
        prepare(d)

        @pl.when(k > 1)
        def _():
            data_copy(peer_of(me, k - 1)).start()

        return c

    lax.fori_loop(1, shards, send_data, 0)
    for j in range(4):
        x = ready(me, j).astype(jnp.bfloat16)
        first = LANES if j % 2 else 0
        out[j // 2, first:first + x.shape[0], mine] = x
    data_copy(peer_of(me, shards - 1)).start()

    def wait_router(k, c):
        router_from(peer_of(me, k)).wait_recv()
        return c

    lax.fori_loop(1, shards, wait_router, 0)

    def expert_copy(e):
        return pltpu.make_async_remote_copy(
            router.at[ex], router.at[ex], e_send.at[e], e_recv.at[ex], device_id={"expert": e}, device_id_type=MESH)

    def expert_from(e):
        return pltpu.make_async_remote_copy(
            router.at[e], router.at[e], e_send.at[e], e_recv.at[e], device_id={"expert": e}, device_id_type=MESH)

    def send_expert(k, c):
        expert_copy((ex + k) % experts).start()
        return c

    lax.fori_loop(1, experts, send_expert, 0)

    def finish_early(k, c):
        d = peer_of(me, k)
        max_copy(d).wait_send()
        scale_copy(d).wait_send()
        router_copy(d).wait_send()
        return c

    lax.fori_loop(1, shards, finish_early, 0)

    def finish_expert(k, c):
        e = (ex + k) % experts
        expert_copy(e).wait_send()
        expert_from(e).wait_recv()
        return c

    lax.fori_loop(1, experts, finish_expert, 0)

    def finish(k, c):
        d = peer_of(me, k)
        data_copy(d).wait_send()
        data_from(d).wait_recv()
        return c

    lax.fori_loop(1, shards, finish, 0)


def store(out_in, scale_in, router_in, out, scale, router, columns, sem):
    rows = out.shape[1]
    copies = [pltpu.make_async_copy(out_in.at[e], out.at[e], sem.at[e]) for e in range(2)]
    for copy in copies:
        copy.start()
    keep = pltpu.make_async_copy(scale_in, scale, sem.at[2])
    keep.start()
    for e in range(router_in.shape[0]):
        columns[2 * e:2 * e + 2, :] = router_in[e]
    last = pltpu.make_async_copy(columns, router, sem.at[3])
    last.start()
    for copy in (*copies, keep, last):
        copy.wait()


def per_device(train_down, other_down, router_weight, router_gain):
    shards, experts = lax.axis_size("shard"), lax.axis_size("expert")
    each, length, width = train_down.shape
    rows = length // shards
    vmem = pl.BlockSpec(memory_space=pltpu.VMEM)
    hbm = pl.BlockSpec(memory_space=pl.ANY)
    bf16, f32 = jnp.bfloat16, jnp.float32
    dma = pltpu.SemaphoreType.DMA
    blocks = (4, LANES)
    out, scale, router = pl.pallas_call(
        exchange,
        out_shape=(
            jax.ShapeDtypeStruct((each, rows, width * shards), bf16),
            jax.ShapeDtypeStruct((each, rows), f32),
            jax.ShapeDtypeStruct((experts, each, shards * LANES), bf16),
        ),
        in_specs=[hbm, hbm, vmem, vmem],
        out_specs=(vmem, vmem, vmem),
        scratch_shapes=[
            pltpu.VMEM((each, length, width), f32),
            pltpu.VMEM((each, length, width), bf16),
            pltpu.VMEM((shards, each, rows, width), bf16),
            pltpu.VMEM((shards, *blocks), f32),
            pltpu.VMEM((shards, *blocks), f32),
            pltpu.VMEM(blocks, f32),
            pltpu.VMEM((shards, *blocks), f32),
            dma((2, 8)),
            *[dma((shards,)) for _ in range(8)],
            dma((experts,)),
            dma((experts,)),
        ],
        compiler_params=pltpu.CompilerParams(
            collective_id=0, has_side_effects=True, vmem_limit_bytes=48 * 1024 * 1024
        ),
        name="exchange",
    )(train_down, other_down, router_weight.T, router_gain.reshape(1, LANES))
    out, scale, router = pl.pallas_call(
        store,
        out_shape=(
            jax.ShapeDtypeStruct(out.shape, bf16),
            jax.ShapeDtypeStruct(scale.shape, f32),
            jax.ShapeDtypeStruct((experts * each, shards * LANES), bf16),
        ),
        in_specs=[vmem] * 3,
        out_specs=[hbm] * 3,
        scratch_shapes=[pltpu.VMEM((experts * each, shards * LANES), bf16), dma((4,))],
        compiler_params=pltpu.CompilerParams(vmem_limit_bytes=8 * 1024 * 1024),
        name="store",
    )(out, scale, router)
    return out, scale, router.T


def solution(mesh):
    in_specs = (
        P("expert", None, "shard"),
        P("expert", None, "shard"),
        P("shard", "expert"),
        P("shard"),
    )
    out_specs = (P("expert", "shard", None), P("expert", "shard"), P())
    return jax.shard_map(
        per_device, mesh=mesh, in_specs=in_specs, out_specs=out_specs, check_vma=False
    )
```

time: 202 us -> 100 us (0.50)
  Pallas kernels: 0 us -> 97.1 us
  waiting for transfers between devices: 77.9 us -> 0 us
  blocking collectives: 47.7 us -> 0 us
  local copies, waits for them, and re-layouts: 39.7 us -> 1.33 us
  starting transfers between devices: 21.3 us -> 0 us
  other arithmetic: 12.9 us -> 0 us
    pallas_call x0 -> x2, Pallas kernels: none -> 97.1 us  [the longest x1 95.3 us: per_device(): pl.pallas_call(exchange, out_shape=(jax.ShapeDtypeStruct((each, rows, wid...]
    all_to_all x3 -> x0, waiting for transfers between devices: 77.9 us -> none  [the longest x1 75.6 us: per_device(): lax.all_to_all(narrow_down, 'shard', split_axis=1, concat_axis=2, tiled=T...]
    all_to_all x1 -> x0, blocking collectives: 47.7 us -> none  [sent_to_all(): return lax.all_to_all(copies, axis, split_axis=0, concat_axis=0, tiled=True)]
    convert_element_type x1 -> x0, local copies, waits for them, and re-layouts: 27.9 us -> none  [per_device(): (latest_down / jnp.expand_dims(scale_down, 2)).astype(jnp.bfloat16)]
    all_to_all x3 -> x0, starting transfers between devices: 21.3 us -> none  [the longest x2 15.8 us: sent_to_all(): return lax.all_to_all(copies, axis, split_axis=0, concat_axis=0, tiled=True)]
    all_to_all x2 -> x0, local copies, waits for them, and re-layouts: 8.72 us -> none  [per_device(): lax.all_to_all(narrow_down, 'shard', split_axis=1, concat_axis=2, tiled=T...]
    reduce_max x2 -> x0, other arithmetic: 7.51 us -> none  [the longest x1 5.6 us: per_device(): scale_down = of_everyone(jnp.max(jnp.abs(latest_down), axis=2), 'shard')]
    convert_element_type x2 -> x0, other arithmetic: 5.43 us -> none  [the longest x1 4.74 us: per_device(): (latest_down / jnp.expand_dims(scale_down, 2)).astype(jnp.bfloat16)]
  transfers between devices with their start and end apart: 3 -> 0, of which waited for: 2 -> 0; matrix products, arithmetic and copies ran while one was open for 21% -> 0% of each run, Pallas kernels for 0% -> 0%
where the time goes in v1:
time: 100 us; the launch traced here: 99.1 us
  Pallas kernels  97.1 us (97%)
  local copies, waits for them, and re-layouts  1.33 us (1%)
    pallas_call x1, Pallas kernels, per_device(): pl.pallas_call(exchange, out_shape=(jax.ShapeDtypeStruct((each, rows, wid...  95.3 us

profile of v1, /device:TPU:24, one launch (start us, length us, event | category | flops | bytes accessed | tf_op | source)
XLA Modules:
  0.0 99.1 jit_solution(3372182660382226029)
XLA Ops:
  0.6 0.0 copy-start
  0.6 0.7 copy-done
  1.3 0.0 copy-start.1
  1.3 0.7 copy-done.1
  2.0 95.3 %exchange.1 = (bf16[2,200,4096]{2,1,0:T(8,128)(2,1)S(1)}, f32[2,200]{1,0:T(2,128)S(1)}, bf16[8,2,4096]{2,1,0:T(2,128)(2,1)S(1)}) custom-call(f32[2,6400,128]{2,1,0:T(8,128)} %train.1, bf16[2,6400,128]{2,1,0:T(8,128)(2,1)} %other.1, f32[2,128]{1,0:T(2,128)S(1)} %bitcast.3, f32[1,128]{1,0:T(1,128)S(1)} %bitcast.4), custom_call_target="tpu_custom_call" | custom-call | tf_op jit(solution)/shard_map/exchange/pallas_call | solution.py:253
  97.3 1.8 %store.1 = (bf16[2,200,4096]{2,1,0:T(8,128)(2,1)}, f32[2,200]{1,0:T(2,128)}, bf16[16,4096]{1,0:T(8,128)(2,1)}) custom-call(bf16[2,200,4096]{2,1,0:T(8,128)(2,1)S(1)} %get-tuple-element.9.out_in, f32[2,200]{1,0:T(2,128)S(1)} %get-tuple-element.10.scale_in, bf16[8,2,4096]{2,1,0:T(2,128)(2,1)S(1)} %get-tuple-element.11.router_in), custom_call_target="tpu_custom_call" | custom-call | tf_op jit(solution)/shard_map/store/pallas_call | solution.py:280
Async XLA Ops:
  0.6 0.7 copy-start
  1.3 0.7 copy-start.1
